TPU v7x, 32 devices: a whole 2x2x4 slice. The times are simulated.
32 devices in a mesh: grp: 2 (over x), tok: 8 (over z, y), side: 2 (over core).
Axes of the slice: x: 2, y: 2, z: 4, core: 2. Of those that a mesh axis runs over, the one named last changes fastest.
Arguments:
- hidden_in: bfloat16 [512, 3072], P(('grp', 'tok')), parts along dimension 0, may hold values from -6 to 6
- queries: bfloat16 [512, 24, 128], P(('grp', 'tok'), 'side'), parts along dimension 0, may hold values from -32 to 32
- key_new: bfloat16 [512, 4, 128], P(('grp', 'tok'), 'side'), parts along dimension 0, may hold values from -32 to 32
- value_new: bfloat16 [512, 4, 128], P(('grp', 'tok'), 'side'), parts along dimension 0, may hold values from -6 to 6
- cache_keys: bfloat16 [512, 4, 128, 128], P(('grp', 'tok'), 'side'), parts along dimension 0, may hold values from -32 to 32
- cache_values: bfloat16 [512, 4, 128, 128], P(('grp', 'tok'), 'side'), parts along dimension 0, may hold values from -6 to 6
- lengths: int32 [512], P(('grp', 'tok')), parts along dimension 0, may hold values from 1 to 128, 16384 in all
- out_weight: bfloat16 [3072, 3072], P('side', 'tok'), may hold values from -0.109375 to 0.109375
- norm_gain: float32 [3072], replicated, may hold values from 0.1 to 1.9
- router_weight: float32 [3072, 4], replicated, may hold values from -0.109375 to 0.109375
- gate_weight: bfloat16 [3072, 32768], P(None, ('tok', 'side')), may hold values from -0.109375 to 0.109375
- up_weight: bfloat16 [3072, 32768], P(None, ('tok', 'side')), may hold values from -0.109375 to 0.109375
- down_weight: bfloat16 [32768, 3072], P(('tok', 'side')), may hold values from -0.0625 to 0.0625
- routes: int32 [512, 2], P('grp'), parts along dimension 0, may hold values from 0 to 3, all different within a row; in each aligned block of 32 rows (0 to 31, 32 to 63, ...) at most 24 rows name the same one
Outputs:
- mixed: bfloat16 [512, 3072], P(('grp', 'tok')), parts along dimension 0
There are 2 independent parts, one for each index of `grp`. A program takes and returns all parts, laid end to end along the dimension named above; an argument that names none is the same for every part. Nothing has to cross between parts.
Inputs may be any that keep to these rules, and one draw needn't show every extreme that they name: Every sequence has at least one valid cache position and some sequence has 128; in each serving group the lengths sum to 16384. `routes`: each row names two different experts; among the rows of one index of tok (aligned blocks of 32 rows) no expert is named by more than 24 rows, and some expert reaches 24 in some block.
All inputs are finite; a program needn't handle non-finite values.
Results may differ from a plain program's by a relative error of at most 0.0075.
Values may be sent and summed in bfloat16 or wider, within the bound.
No kernel may reach another device: no remote copies, remote signals or barrier semaphores. Data moves between devices by JAX's collectives and lax.ppermute only.
A program may use at most 128 MiB of HBM per device.

v0:
```python
import math
import jax
import jax.numpy as jnp
from jax import lax
from jax.sharding import PartitionSpec as P

CAP = 24


def attend(queries, key_new, value_new, cache_keys, cache_values, lengths):
    seq_count, head_count, head_width = queries.shape
    kv_count = key_new.shape[1]
    places = cache_keys.shape[2]
    scaling = 1.0 / math.sqrt(head_width)
    grouped = queries.reshape(seq_count, kv_count, head_count // kv_count, head_width)
    scores = (
        jnp.einsum("skgd,skpd->skgp", grouped, cache_keys, preferred_element_type=jnp.float32)
        * scaling
    )
    usable = jnp.arange(places, dtype=jnp.int32)[None, :] < lengths[:, None]
    scores = jnp.where(usable[:, None, None, :], scores, -jnp.inf)
    own_score = (
        jnp.einsum("skgd,skd->skg", grouped, key_new, preferred_element_type=jnp.float32) * scaling
    )
    top_score = jnp.maximum(jnp.max(scores, axis=-1), own_score)
    weights = jnp.exp(scores - top_score[..., None])
    own_weight = jnp.exp(own_score - top_score)
    totals = jnp.sum(weights, axis=-1) + own_weight
    prob_low = (weights / totals[..., None]).astype(jnp.bfloat16)
    own_low = (own_weight / totals).astype(jnp.bfloat16)
    mixture = jnp.einsum(
        "skgp,skpd->skgd", prob_low, cache_values, preferred_element_type=jnp.float32
    )
    mixture = (
        mixture
        + own_low.astype(jnp.float32)[..., None] * value_new.astype(jnp.float32)[:, :, None, :]
    )
    return mixture.astype(jnp.bfloat16).reshape(seq_count, head_count * head_width)


def gating(normed, chosen, router_weight):
    logits = jnp.dot(normed.astype(jnp.float32), router_weight, precision=lax.Precision.HIGHEST)
    expert_ids = jnp.arange(router_weight.shape[1], dtype=jnp.int32)
    picks = (chosen[:, :, None] == expert_ids[None, None, :]).astype(jnp.float32)
    chosen_logits = jnp.sum(picks * logits[:, None, :], axis=-1)
    leading = jax.nn.sigmoid(chosen_logits[:, 0] - chosen_logits[:, 1])
    gates = jnp.stack([leading, 1.0 - leading], axis=1)
    return (gates, picks)


def expert_rows(block, gate_weight, up_weight, down_weight):
    gated = jnp.dot(block, gate_weight, preferred_element_type=jnp.float32)
    upward = jnp.dot(block, up_weight, preferred_element_type=jnp.float32)
    active = (jax.nn.silu(gated) * upward).astype(jnp.bfloat16)
    return jnp.dot(active, down_weight, preferred_element_type=jnp.float32)


def local(
    hidden_in,
    queries,
    key_new,
    value_new,
    cache_keys,
    cache_values,
    lengths,
    out_weight,
    norm_gain,
    router_weight,
    gate_weight,
    up_weight,
    down_weight,
    routes,
):
    seq_rows = hidden_in.shape[0]
    model_width = hidden_in.shape[1]
    tok_count = lax.axis_size("tok")
    expert_total = router_weight.shape[1]
    replicas = tok_count // expert_total
    pieces = 1
    rows_each = seq_rows // pieces
    capacity = min(CAP, rows_each)
    first_row = lax.axis_index("tok") * seq_rows
    attn_out = attend(queries, key_new, value_new, cache_keys, cache_values, lengths)
    columns = jnp.dot(
        lax.all_gather(attn_out, "tok", axis=0, tiled=True),
        out_weight,
        preferred_element_type=jnp.float32,
    )
    partial_out = lax.all_to_all(columns, "tok", split_axis=0, concat_axis=1, tiled=True)
    projected = lax.psum(partial_out, "side")
    stream = (hidden_in.astype(jnp.float32) + projected).astype(jnp.bfloat16).astype(jnp.float32)
    normed = (
        stream * lax.rsqrt(jnp.mean(stream * stream, axis=-1, keepdims=True) + 1e-05) * norm_gain
    ).astype(jnp.bfloat16)
    chosen = lax.dynamic_slice_in_dim(routes, first_row + 0, rows_each, 0)
    gates, picks = gating(normed, chosen, router_weight)
    hits = jnp.sum(picks, axis=1)
    ranks = jnp.cumsum(hits, axis=0) - hits
    slot_ids = jnp.arange(capacity, dtype=jnp.float32)
    placed = hits[:, :, None] * (ranks[:, :, None] == slot_ids[None, None, :]).astype(jnp.float32)
    send_rows = jnp.einsum(
        "bec,bd->ecd", placed.astype(jnp.bfloat16), normed, preferred_element_type=jnp.float32
    ).astype(jnp.bfloat16)
    outgoing = jnp.repeat(send_rows, replicas, axis=0)
    arrived = lax.all_to_all(outgoing, "tok", split_axis=0, concat_axis=0, tiled=True)
    sources, slots, width_in = arrived.shape
    partial_rows = expert_rows(
        arrived.reshape(sources * slots, width_in), gate_weight, up_weight, down_weight
    )
    returned = lax.all_to_all(
        partial_rows.reshape(sources, slots, width_in),
        "tok",
        split_axis=0,
        concat_axis=0,
        tiled=True,
    )
    per_expert = jnp.sum(returned.reshape(expert_total, replicas, capacity, model_width), axis=1)
    slot_gates = (
        jnp.einsum("bk,bke->be", gates, picks, precision=lax.Precision.HIGHEST)[:, :, None] * placed
    )
    combined = jnp.einsum("bec,ecd->bd", slot_gates, per_expert, precision=lax.Precision.HIGHEST)
    combined_all = lax.psum(combined, "side")
    results = (stream + combined_all).astype(jnp.bfloat16)
    return results


def solution(mesh):
    return jax.shard_map(
        local,
        mesh=mesh,
        in_specs=(
            P(("grp", "tok"), None),
            P(("grp", "tok"), "side", None),
            P(("grp", "tok"), "side", None),
            P(("grp", "tok"), "side", None),
            P(("grp", "tok"), "side", None, None),
            P(("grp", "tok"), "side", None, None),
            P(("grp", "tok")),
            P("side", "tok"),
            P(),
            P(),
            P(None, ("tok", "side")),
            P(None, ("tok", "side")),
            P(("tok", "side"), None),
            P("grp", None),
        ),
        out_specs=P(("grp", "tok"), None),
        check_vma=False,
    )
```

profile of v0, /device:TPU:0, one launch (start us, length us, event | category | flops | bytes accessed | tf_op | source)
XLA Modules:
  0.0 225.7 jit_solution(1218781161953350367)
XLA Ops:
  6.5 0.0 copy-start
  6.5 0.0 all-reduce.3.cloned.1.call-start
  6.5 0.9 iota_compare_fusion.2
  7.4 0.7 convert_element_type.48
  8.2 1.1 fusion.10
  9.3 0.0 copy-done
  9.3 0.0 copy-start.5
  9.3 2.3 %fusion.31 = (f32[32,2,6]{2,1,0:T(2,128)S(1)}, f32[32,2,6,128]{3,2,1,0:T(8,128)S(1)}) fusion(bf16[32,2,128,128]{3,2,1,0:T(8,128)(2,1)S(1)} %copy-done, bf16[32,2,6,128]{3,0,2,1:T(8,128)(2,1)} %bitcast.37, pred[32,128]{1,0:T(8,128)(4,1)S(1)} %iota_compare_fusion.2), kind=kOutput, calls=%fused_computation.57 | convolution fusion | flops 12729984 | bytes 2397696 | tf_op jit(solution)/shard_map/skgd,skpd->skgp/dot_general | solution.py:17
  11.7 0.3 fusion.8
  11.9 0.1 fusion.30
  12.0 0.0 copy-done.5
  12.0 0.0 copy-start.1
  12.0 0.7 fusion.2
  12.7 0.1 reshape.65
  12.9 33.8 %all_gather.3 = bf16[256,1536]{1,0:T(8,128)(2,1)S(1)} all-gather(bf16[32,1536]{1,0:T(8,128)(2,1)S(1)} %reshape.65), channel_id=1, replica_groups=mesh['grp'=2,'tok'=8,'side'=2] {'tok'}, dimensions={0}, use_global_device_ids=true | all-gather | bytes 884736 | tf_op jit(solution)/shard_map/all_gather | solution.py:85
  46.7 0.0 copy-done.1
  46.7 0.6 fusion.32
  47.2 0.0 copy-start.4
  47.3 0.0 copy-start.2
  47.3 0.0 copy-start.3
  47.3 0.0 copy-start.6
  47.3 14.9 %all_to_all.29 = f32[8,32,384]{2,1,0:T(8,128)S(1)} all-to-all(f32[8,32,384]{2,1,0:T(8,128)S(1)} %bitcast.32), channel_id=1, replica_groups=mesh['grp'=2,'tok'=8,'side'=2] {'tok'}, dimensions={0} | all-to-all | bytes 786432 | tf_op jit(solution)/shard_map/all_to_all | solution.py:89
  62.2 0.8 copy.45
  63.0 0.0 all-reduce.3.cloned.1.call-update
  63.0 0.0 all-reduce.5.cloned.1.call-start
  63.1 0.0 copy-done.4
  63.1 0.1 constant_dynamic-slice_fusion
  63.2 16.9 %all-reduce.3.cloned.1.call-done = f32[32,3072]{1,0:T(8,128)} async-done(((f32[32,3072]{1,0:T(8,128)}), f32[32,3072]{1,0:T(8,128)}) %all-reduce.3.cloned.1.call-update) | async-done | bytes 393232 | tf_op jit(solution)/shard_map/psum | solution.py:90
  80.1 0.0 copy-done.2
  80.1 1.2 fusion.4
  81.3 0.0 copy-done.3
  81.3 0.0 copy-done.6
  81.3 0.3 fusion.16
  81.7 0.1 copy.35
  81.8 0.1 reduce_window_sum.11
  81.9 0.1 copy.37
  82.0 0.4 convolution_convert_fusion
  82.3 0.1 broadcast_in_dim.16
  82.5 34.9 %all_to_all.30 = bf16[8,24,3072]{2,1,0:T(8,128)(2,1)S(1)} all-to-all(bf16[8,24,3072]{2,1,0:T(8,128)(2,1)S(1)} %bitcast.29), channel_id=1, replica_groups=mesh['grp'=2,'tok'=8,'side'=2] {'tok'}, dimensions={0} | all-to-all | bytes 2359296 | tf_op jit(solution)/shard_map/all_to_all | solution.py:105
  117.4 8.4 %fusion.33 = f32[192,2048]{1,0:T(8,128)} fusion(bf16[192,3072]{1,0:T(8,128)(2,1)S(1)} %bitcast.34, bf16[3072,2048]{1,0:T(8,128)(2,1)} %param.24), kind=kOutput, calls=%fused_computation.59 | convolution fusion | flops 2415919104 | bytes 15335424 | tf_op jit(solution)/shard_map/dot_general | solution.py:52
  125.8 15.3 %fusion.3 = f32[192,3072]{1,0:T(8,128)} fusion(bf16[2048,3072]{1,0:T(8,128)(2,1)} %param.26, bf16[192,3072]{1,0:T(8,128)(2,1)S(1)} %bitcast.35, bf16[3072,2048]{1,0:T(8,128)(2,1)} %param.25, f32[192,2048]{1,0:T(8,128)} %fusion.33), kind=kOutput, calls=%fused_computation.9 | convolution fusion | flops 4834197504 | bytes 30277632 | tf_op jit(solution)/shard_map/dot_general | solution.py:55
  141.1 57.0 %all_to_all.31 = f32[8,24,3072]{2,1,0:T(8,128)S(1)} all-to-all(f32[8,24,3072]{2,1,0:T(8,128)} %bitcast.30), channel_id=1, replica_groups=mesh['grp'=2,'tok'=8,'side'=2] {'tok'}, dimensions={0} | all-to-all | bytes 4718592 | tf_op jit(solution)/shard_map/all_to_all | solution.py:110
  198.1 0.1 bitcast_reduce_fusion
  198.3 1.5 convolution_bitcast_fusion
  199.7 0.0 all-reduce.5.cloned.1.call-update
  199.7 17.5 %all-reduce.5.cloned.1.call-done = f32[32,3072]{1,0:T(8,128)} async-done(((f32[32,3072]{1,0:T(8,128)}), f32[32,3072]{1,0:T(8,128)}) %all-reduce.5.cloned.1.call-update) | async-done | bytes 393232 | tf_op jit(solution)/shard_map/psum | solution.py:122
  217.2 1.7 fusion.7
  (7 shorter events, 0.1 us)
Async XLA Ops:
  6.5 2.7 %copy-start = (bf16[32,2,128,128]{3,2,1,0:T(8,128)(2,1)S(1)}, bf16[32,2,128,128]{3,2,1,0:T(8,128)(2,1)}, u32[]{:S(2)}) copy-start(bf16[32,2,128,128]{3,2,1,0:T(8,128)(2,1)} %param.18) | copy-start | bytes 6291460
  6.5 73.6 %all-reduce.3.cloned.1.call-start = ((), (), s32[]{:S(2)}) async-start(), calls=%async_computation.3 | async-start | bytes 786432 | tf_op jit(solution)/shard_map/psum | solution.py:90
  9.3 2.7 %copy-start.5 = (bf16[32,2,128,128]{3,2,1,0:T(8,128)(2,1)S(1)}, bf16[32,2,128,128]{3,2,1,0:T(8,128)(2,1)}, u32[]{:S(2)}) copy-start(bf16[32,2,128,128]{3,2,1,0:T(8,128)(2,1)} %param.19) | copy-start | bytes 6291460
  12.0 34.7 %copy-start.1 = (bf16[1536,384]{1,0:T(8,128)(2,1)S(1)}, bf16[1536,384]{1,0:T(8,128)(2,1)}, u32[]{:S(2)}) copy-start(bf16[1536,384]{1,0:T(8,128)(2,1)} %param.21) | copy-start | bytes 3538948
  47.2 15.8 %copy-start.4 = (s32[256,2]{0,1:T(2,128)S(1)}, s32[256,2]{0,1:T(2,128)}, u32[]{:S(2)}) copy-start(s32[256,2]{0,1:T(2,128)} %param.27) | copy-start | bytes 6148
  47.3 32.9 %copy-start.2 = (bf16[32,3072]{1,0:T(8,128)(2,1)S(1)}, bf16[32,3072]{1,0:T(8,128)(2,1)}, u32[]{:S(2)}) copy-start(bf16[32,3072]{1,0:T(8,128)(2,1)} %param.14) | copy-start | bytes 589828
  47.3 34.0 %copy-start.3 = (f32[3072]{0:T(1024)S(1)}, f32[3072]{0:T(1024)}, u32[]{:S(2)}) copy-start(f32[3072]{0:T(1024)} %param.22) | copy-start | bytes 36868
  47.3 34.0 %copy-start.6 = (f32[3072,4]{0,1:T(4,128)S(1)}, f32[3072,4]{0,1:T(4,128)}, u32[]{:S(2)}) copy-start(f32[3072,4]{0,1:T(4,128)} %param.23) | copy-start | bytes 147460
  63.0 154.2 %all-reduce.5.cloned.1.call-start = ((), (), s32[]{:S(2)}) async-start(), calls=%async_computation.4 | async-start | bytes 786432 | tf_op jit(solution)/shard_map/psum | solution.py:122
Sparse Core Ops, SparseCore 0:
  63.1 16.9 all-reduce.2
  199.9 17.2 all-reduce.4
where the time goes:
time: 226 us
  blocking collectives  141 us (62%)
  waiting for transfers between devices  34.4 us (15%)
  matrix products  30.5 us (13%)
  between operations  13.6 us (6%)
  other arithmetic  5.14 us (2%)
    all_to_all x1, blocking collectives, local(): lax.all_to_all(partial_rows.reshape(sources, slots, width_in), 'tok', spl...  57 us
    all_to_all x1, blocking collectives, local(): lax.all_to_all(outgoing, 'tok', split_axis=0, concat_axis=0, tiled=True)  34.9 us
    all_gather x1, blocking collectives, local(): lax.all_gather(attn_out, 'tok', axis=0, tiled=True)  33.8 us
    psum x1, waiting for transfers between devices, local(): combined_all = lax.psum(combined, 'side')  17.5 us
    psum x1, waiting for transfers between devices, local(): projected = lax.psum(partial_out, 'side')  16.9 us
    dot_general x1, matrix products, expert_rows(): return jnp.dot(active, down_weight, preferred_element_type=jnp.float32)  15.3 us
    all_to_all x1, blocking collectives, local(): lax.all_to_all(columns, 'tok', split_axis=0, concat_axis=1, tiled=True)  14.9 us
    dot_general x1, matrix products, expert_rows(): gated = jnp.dot(block, gate_weight, preferred_element_type=jnp.float32)  8.39 us
  transfers between devices with their start and end apart: 2, of which 2 were waited for; matrix products, arithmetic and copies ran while one was open for 0% of the time, Pallas kernels for 0%

commit v1 on v0

--- a/solution.py
+++ b/solution.py
@@ -119,7 +119,7 @@
         jnp.einsum("bk,bke->be", gates, picks, precision=lax.Precision.HIGHEST)[:, :, None] * placed
     )
     combined = jnp.einsum("bec,ecd->bd", slot_gates, per_expert, precision=lax.Precision.HIGHEST)
-    combined_all = lax.psum(combined, "side")
+    combined_all = jnp.sum(lax.all_gather(combined, "side"), axis=0)
     results = (stream + combined_all).astype(jnp.bfloat16)
     return results
 

time: 226 us -> 209 us (0.925)
  waiting for transfers between devices: 34.4 us -> 17 us
    psum x1 -> x0, waiting for transfers between devices: 17.5 us -> none  [local(): combined_all = lax.psum(combined, 'side')]
    all_gather x0 -> x1, blocking collectives: none -> 2.37 us  [local(): combined_all = jnp.sum(lax.all_gather(combined, 'side'), axis=0)]
  transfers between devices with their start and end apart: 2 -> 1, of which waited for: 2 -> 1; matrix products, arithmetic and copies ran while one was open for 0% -> 0% of each run, Pallas kernels for 0% -> 0%
where the time goes in v1:
time: 209 us
  blocking collectives  143 us (68%)
  matrix products  29.8 us (14%)
  waiting for transfers between devices  17 us (8%)
  between operations  13.6 us (7%)
  other arithmetic  4.18 us (2%)
    all_to_all x1, blocking collectives, local(): lax.all_to_all(partial_rows.reshape(sources, slots, width_in), 'tok', spl...  57 us
    all_to_all x1, blocking collectives, local(): lax.all_to_all(outgoing, 'tok', split_axis=0, concat_axis=0, tiled=True)  34.9 us
    all_gather x1, blocking collectives, local(): lax.all_gather(attn_out, 'tok', axis=0, tiled=True)  33.8 us
    psum x1, waiting for transfers between devices, local(): projected = lax.psum(partial_out, 'side')  17 us
    dot_general x1, matrix products, expert_rows(): return jnp.dot(active, down_weight, preferred_element_type=jnp.float32)  15.3 us
    all_to_all x1, blocking collectives, local(): lax.all_to_all(columns, 'tok', split_axis=0, concat_axis=1, tiled=True)  14.9 us
    dot_general x1, matrix products, expert_rows(): gated = jnp.dot(block, gate_weight, preferred_element_type=jnp.float32)  8.39 us
  transfers between devices with their start and end apart: 1, of which 1 were waited for; matrix products, arithmetic and copies ran while one was open for 0% of the time, Pallas kernels for 0%

profile of v1, /device:TPU:0, one launch (start us, length us, event | category | flops | bytes accessed | tf_op | source)
XLA Modules:
  0.0 208.9 jit_solution(9393607086888672449)
XLA Ops:
  6.5 0.0 copy-start
  6.5 0.0 all-reduce.2.cloned.1.call-start
  6.5 0.9 iota_compare_fusion.2
  7.4 0.7 convert_element_type.48
  8.2 1.1 fusion.10
  9.3 0.0 copy-done
  9.3 0.0 copy-start.5
  9.3 2.3 %fusion.31 = (f32[32,2,6]{2,1,0:T(2,128)S(1)}, f32[32,2,6,128]{3,2,1,0:T(8,128)S(1)}) fusion(bf16[32,2,128,128]{3,2,1,0:T(8,128)(2,1)S(1)} %copy-done, bf16[32,2,6,128]{3,0,2,1:T(8,128)(2,1)} %bitcast.39, pred[32,128]{1,0:T(8,128)(4,1)S(1)} %iota_compare_fusion.2), kind=kOutput, calls=%fused_computation.57 | convolution fusion | flops 12729984 | bytes 2397696 | tf_op jit(solution)/shard_map/skgd,skpd->skgp/dot_general | solution.py:17
  11.7 0.3 fusion.8
  11.9 0.1 fusion.30
  12.0 0.0 copy-done.5
  12.0 0.0 copy-start.1
  12.0 0.7 fusion.2
  12.7 0.1 reshape.65
  12.9 33.8 %all_gather.9 = bf16[256,1536]{1,0:T(8,128)(2,1)S(1)} all-gather(bf16[32,1536]{1,0:T(8,128)(2,1)S(1)} %reshape.65), channel_id=1, replica_groups=mesh['grp'=2,'tok'=8,'side'=2] {'tok'}, dimensions={0}, use_global_device_ids=true | all-gather | bytes 884736 | tf_op jit(solution)/shard_map/all_gather | solution.py:85
  46.7 0.0 copy-done.1
  46.7 0.6 fusion.32
  47.2 0.0 copy-start.4
  47.3 0.0 copy-start.2
  47.3 0.0 copy-start.3
  47.3 0.0 copy-start.6
  47.3 14.9 %all_to_all.29 = f32[8,32,384]{2,1,0:T(8,128)S(1)} all-to-all(f32[8,32,384]{2,1,0:T(8,128)S(1)} %bitcast.34), channel_id=1, replica_groups=mesh['grp'=2,'tok'=8,'side'=2] {'tok'}, dimensions={0} | all-to-all | bytes 786432 | tf_op jit(solution)/shard_map/all_to_all | solution.py:89
  62.2 0.8 copy.45
  63.0 0.0 all-reduce.2.cloned.1.call-update
  63.0 0.0 copy-done.4
  63.0 0.1 constant_dynamic-slice_fusion
  63.1 17.0 %all-reduce.2.cloned.1.call-done = f32[32,3072]{1,0:T(8,128)} async-done(((f32[32,3072]{1,0:T(8,128)}), f32[32,3072]{1,0:T(8,128)}) %all-reduce.2.cloned.1.call-update) | async-done | bytes 393232 | tf_op jit(solution)/shard_map/psum | solution.py:90
  80.1 0.0 copy-done.2
  80.1 1.2 fusion.4
  81.3 0.0 copy-done.3
  81.3 0.0 copy-done.6
  81.3 0.3 fusion.16
  81.7 0.1 copy.35
  81.8 0.1 reduce_window_sum.11
  81.9 0.1 copy.37
  82.0 0.4 convolution_convert_fusion
  82.3 0.1 broadcast_in_dim.16
  82.5 34.9 %all_to_all.30 = bf16[8,24,3072]{2,1,0:T(8,128)(2,1)S(1)} all-to-all(bf16[8,24,3072]{2,1,0:T(8,128)(2,1)S(1)} %bitcast.30), channel_id=1, replica_groups=mesh['grp'=2,'tok'=8,'side'=2] {'tok'}, dimensions={0} | all-to-all | bytes 2359296 | tf_op jit(solution)/shard_map/all_to_all | solution.py:105
  117.4 8.4 %fusion.33 = f32[192,2048]{1,0:T(8,128)} fusion(bf16[192,3072]{1,0:T(8,128)(2,1)S(1)} %bitcast.36, bf16[3072,2048]{1,0:T(8,128)(2,1)} %param.24), kind=kOutput, calls=%fused_computation.59 | convolution fusion | flops 2415919104 | bytes 15335424 | tf_op jit(solution)/shard_map/dot_general | solution.py:52
  125.8 15.3 %fusion.3 = f32[192,3072]{1,0:T(8,128)} fusion(bf16[2048,3072]{1,0:T(8,128)(2,1)} %param.26, bf16[192,3072]{1,0:T(8,128)(2,1)S(1)} %bitcast.37, bf16[3072,2048]{1,0:T(8,128)(2,1)} %param.25, f32[192,2048]{1,0:T(8,128)} %fusion.33), kind=kOutput, calls=%fused_computation.9 | convolution fusion | flops 4834197504 | bytes 30277632 | tf_op jit(solution)/shard_map/dot_general | solution.py:55
  141.1 57.0 %all_to_all.31 = f32[8,24,3072]{2,1,0:T(8,128)S(1)} all-to-all(f32[8,24,3072]{2,1,0:T(8,128)} %bitcast.32), channel_id=1, replica_groups=mesh['grp'=2,'tok'=8,'side'=2] {'tok'}, dimensions={0} | all-to-all | bytes 4718592 | tf_op jit(solution)/shard_map/all_to_all | solution.py:110
  198.1 0.1 bitcast_reduce_fusion
  198.3 0.7 convolution_bitcast_fusion
  199.0 2.4 %all-gather = f32[64,3072]{1,0:T(8,128)S(1)} all-gather(f32[32,3072]{1,0:T(8,128)S(1)} %convolution_bitcast_fusion), channel_id=2, replica_groups=mesh['grp'=2,'tok'=8,'side'=2] {'side'}, dimensions={0}, use_global_device_ids=true | all-gather | bytes 1179648 | tf_op jit(solution)/shard_map/all_gather | solution.py:122
  201.4 0.7 fusion.7
  (8 shorter events, 0.2 us)
Async XLA Ops:
  6.5 2.7 %copy-start = (bf16[32,2,128,128]{3,2,1,0:T(8,128)(2,1)S(1)}, bf16[32,2,128,128]{3,2,1,0:T(8,128)(2,1)}, u32[]{:S(2)}) copy-start(bf16[32,2,128,128]{3,2,1,0:T(8,128)(2,1)} %param.18) | copy-start | bytes 6291460
  6.5 73.6 %all-reduce.2.cloned.1.call-start = ((), (), s32[]{:S(2)}) async-start(), calls=%async_computation.3 | async-start | bytes 786432 | tf_op jit(solution)/shard_map/psum | solution.py:90
  9.3 2.7 %copy-start.5 = (bf16[32,2,128,128]{3,2,1,0:T(8,128)(2,1)S(1)}, bf16[32,2,128,128]{3,2,1,0:T(8,128)(2,1)}, u32[]{:S(2)}) copy-start(bf16[32,2,128,128]{3,2,1,0:T(8,128)(2,1)} %param.19) | copy-start | bytes 6291460
  12.0 34.7 %copy-start.1 = (bf16[1536,384]{1,0:T(8,128)(2,1)S(1)}, bf16[1536,384]{1,0:T(8,128)(2,1)}, u32[]{:S(2)}) copy-start(bf16[1536,384]{1,0:T(8,128)(2,1)} %param.21) | copy-start | bytes 3538948
  47.2 15.8 %copy-start.4 = (s32[256,2]{0,1:T(2,128)S(1)}, s32[256,2]{0,1:T(2,128)}, u32[]{:S(2)}) copy-start(s32[256,2]{0,1:T(2,128)} %param.27) | copy-start | bytes 6148
  47.3 32.9 %copy-start.2 = (bf16[32,3072]{1,0:T(8,128)(2,1)S(1)}, bf16[32,3072]{1,0:T(8,128)(2,1)}, u32[]{:S(2)}) copy-start(bf16[32,3072]{1,0:T(8,128)(2,1)} %param.14) | copy-start | bytes 589828
  47.3 34.0 %copy-start.3 = (f32[3072]{0:T(1024)S(1)}, f32[3072]{0:T(1024)}, u32[]{:S(2)}) copy-start(f32[3072]{0:T(1024)} %param.22) | copy-start | bytes 36868
  47.3 34.0 %copy-start.6 = (f32[3072,4]{0,1:T(4,128)S(1)}, f32[3072,4]{0,1:T(4,128)}, u32[]{:S(2)}) copy-start(f32[3072,4]{0,1:T(4,128)} %param.23) | copy-start | bytes 147460
Sparse Core Ops, SparseCore 0:
  63.1 16.9 all-reduce.1
